TPU v7x, 512 devices: a whole 4x4x16 slice. The times are simulated.
512 devices in a mesh: gx: 8 (over y, core), gy: 16 (over z), gz: 4 (over x).
Axes of the slice: x: 4, y: 4, z: 16, core: 2. Of those that a mesh axis runs over, the one named last changes fastest.
Arguments:
- a_vals: float32 [16, 16, 4, 6, 128, 128], P('gy', 'gx', 'gz'), may hold values from -0.25 to 0.25
- a_cols: int32 [16, 16, 4, 6], P('gy', 'gx', 'gz'), may hold values from 0 to 63, as said below
- a_count: int32 [16, 16, 4], P('gy', 'gx', 'gz'), may hold values from 1 to 6, as said below
- p_vals: float32 [4, 64, 8, 1, 128, 128], P('gz', 'gy', 'gx'), may hold values from -6 to 6
- p_cols: int32 [4, 64, 8, 1], P('gz', 'gy', 'gx'), may hold values from 0 to 1, as said below
- p_count: int32 [4, 64, 8], P('gz', 'gy', 'gx'), may hold values from 0 to 1, as said below
Outputs:
- c_tiles: float32 [32768, 2048], P(('gy', 'gz'), 'gx')
Inputs may be any that keep to these rules, and one draw needn't show every extreme that they name: `a_cols`: inner tile indices of one block row and slice are distinct across its 6 slots. Slots 0 to a_count - 1 are live; the block rows of every device include one with all 6 slots live. `p_cols`: column tiles of one block row and group are distinct across its 1 slots. Slots 0 to p_count - 1 are live; the block rows of every device include one with all 1 slots live.
All inputs are finite; a program needn't handle non-finite values.
Results may differ from a plain program's by a relative error of at most 0.0003.
Values sent between devices are 32-bit elements; how exact they have to be, the bound alone decides.
A program may use at most 128 MiB of HBM per device.

v0:
```python
import jax
import jax.numpy as jnp
from jax import lax
from jax.sharding import PartitionSpec as P

COLS_DEV = 2


HIGHEST = lax.Precision.HIGHEST


def cut_along(shard, dim, peers):
    shape = shard.shape
    blocks = shard.reshape(*shape[:dim], peers, shape[dim] // peers, *shape[dim + 1 :])
    return jnp.moveaxis(blocks, dim, 0)


def sent_and_summed(shard, axis, dim):
    blocks = cut_along(shard, dim, lax.axis_size(axis))
    arrived = lax.all_to_all(blocks, axis, split_axis=0, concat_axis=0, tiled=True)
    return arrived.sum(axis=0)


def placement_weights(counts, columns, column_tiles):
    slot_total = columns.shape[-1]
    alive_slots = jnp.arange(slot_total, dtype=jnp.int32) < counts[..., None]
    matches = columns[..., None] == jnp.arange(column_tiles, dtype=jnp.int32)
    return (alive_slots[..., None] & matches).astype(jnp.float32)


def body(a_vals, a_cols, a_count, p_vals, p_cols, p_count):
    tile_size = a_vals.shape[-1]
    slots_a = a_vals.shape[3]
    alive_a = jnp.arange(slots_a, dtype=jnp.int32) < a_count[..., None]
    a_masked = jnp.where(alive_a[..., None, None], a_vals, 0.0)
    weights = placement_weights(p_count, p_cols, COLS_DEV)
    strip_width = COLS_DEV * tile_size
    values_all, weights_all = (
        lax.all_gather(p_vals, "gy", axis=1, tiled=True),
        lax.all_gather(weights, "gy", axis=1, tiled=True),
    )
    values_all = values_all[0, :, 0]
    weights_all = weights_all[0, :, 0]
    tile_part = lax.all_gather(a_masked, "gx", axis=1, tiled=True)
    columns = lax.all_gather(a_cols, "gx", axis=1, tiled=True)
    row_count = tile_part.shape[1]
    block_tile_part = tile_part[0, :, 0]
    indices = columns[0, :, 0]
    chosen = values_all[indices]
    product = jnp.einsum("nsij,nspjk->nspik", block_tile_part, chosen, precision=HIGHEST)
    placed = jnp.einsum("nspc,nspik->nick", weights_all[indices], product, precision=HIGHEST)
    block = placed.reshape(placed.shape[0], tile_size, strip_width).reshape(
        row_count * tile_size, strip_width
    )
    return sent_and_summed(block, "gz", 0)


def solution(mesh):
    placed = (
        P("gy", "gx", "gz", None, None, None),
        P("gy", "gx", "gz", None),
        P("gy", "gx", "gz"),
        P("gz", "gy", "gx", None, None, None),
        P("gz", "gy", "gx", None),
        P("gz", "gy", "gx"),
    )
    return jax.shard_map(
        body, mesh=mesh, in_specs=placed, out_specs=P(("gy", "gz"), "gx"), check_vma=False
    )
```

profile of v0, /device:TPU:1, one launch (start us, length us, event | category | flops | bytes accessed | tf_op | source)
XLA Modules:
  0.0 213.5 jit_solution(4580665249388284222)
XLA Ops:
  6.5 0.0 all-gather.3.cloned.1.call-start
  6.5 0.7 all-gather.3.cloned.1.call-update
  7.3 0.0 all-gather.5.cloned.1.call-start
  7.3 0.7 iota_compare_fusion
  8.0 2.2 %bitcast_select_fusion = f32[1,2,1,6,128,128]{5,4,3,2,0,1:T(8,128)} fusion(f32[1,2,1,6,128,128]{5,4,3,2,1,0:T(8,128)} %param.6, pred[2,6]{1,0:T(4,128)(4,1)S(1)} %iota_compare_fusion), kind=kLoop, calls=%fused_computation.6 | loop fusion | flops 196608 | bytes 1572876 | tf_op jit(solution)/shard_map/jit(_where)/select_n | solution.py:35
  10.2 0.0 all-gather.5.cloned.1.call-update
  10.2 14.8 %all_gather.13 = s32[1,16,1,6]{3,2,0,1:T(1,128)S(1)} all-gather(s32[1,2,1,6]{3,2,0,1:T(1,128)} %bitcast.38), channel_id=1, replica_groups=mesh['gx'=8,'gy'=16,'gz'=4] {'gx'}, dimensions={1}, use_global_device_ids=true | all-gather | bytes 432 | tf_op jit(solution)/shard_map/all_gather | solution.py:45
  25.0 0.1 copy.24
  25.1 0.1 copy.25
  25.2 0.1 reshape.152
  25.3 0.7 compare_bitcast_fusion
  26.0 0.7 and_convert_fusion
  26.7 28.2 %all_gather.15 = f32[1,64,1,1,2]{4,3,2,0,1:T(1,128)S(1)} all-gather(f32[1,4,1,1,2]{4,3,2,0,1:T(1,128)S(1)} %and_convert_fusion), channel_id=1, replica_groups=mesh['gx'=8,'gy'=16,'gz'=4] {'gy'}, dimensions={1}, use_global_device_ids=true | all-gather | bytes 544 | tf_op jit(solution)/shard_map/all_gather | solution.py:40
  54.9 0.6 gather_fusion.1
  55.5 0.1 copy.30
  55.6 0.1 reshape.147
  55.6 27.7 %all-gather.3.cloned.1.call-done = f32[1,64,1,1,128,128]{5,4,3,2,0,1:T(8,128)} async-done(((f32[1,4,1,1,128,128]{5,4,3,2,0,1:T(8,128)}), f32[1,64,1,1,128,128]{5,4,3,2,0,1:T(8,128)}) %all-gather.3.cloned.1.call-update) | async-done | bytes 4194320 | tf_op jit(solution)/shard_map/all_gather | solution.py:39
  83.4 5.8 %gather_fusion = f32[96,128,128]{2,1,0:T(8,128)} fusion(f32[64,128,128]{2,1,0:T(8,128)} %bitcast.35, s32[1024]{0:T(1024)S(1)} %pad_clamp_fusion), kind=kCustom, calls=%fused_computation | custom fusion | bytes 12583296 | tf_op jit(solution)/shard_map/gather | solution.py:49
  89.2 51.1 %all-gather.5.cloned.1.call-done = f32[1,16,1,6,128,128]{5,4,3,2,0,1:T(8,128)} async-done(((f32[1,2,1,6,128,128]{5,4,3,2,0,1:T(8,128)}), f32[1,16,1,6,128,128]{5,4,3,2,0,1:T(8,128)}) %all-gather.5.cloned.1.call-update) | async-done | bytes 6291472 | tf_op jit(solution)/shard_map/all_gather | solution.py:44
  140.3 14.8 %fusion.2 = f32[16,6,128,128]{2,3,1,0:T(8,128)} fusion(f32[16,6,128,128]{3,2,1,0:T(8,128)} %bitcast.33, f32[1,16,1,6,128,128]{5,4,3,2,0,1:T(8,128)} %all-gather.5.cloned.1.call-done), kind=kOutput, calls=%fused_computation.4 | convolution fusion | flops 2415919104 | bytes 18874368 | tf_op jit(solution)/shard_map/nsij,nspjk->nspik/dot_general | solution.py:50
  155.0 8.4 %copy.31 = f32[16,6,128,128]{3,1,2,0:T(8,128)} copy(f32[16,6,128,128]{2,3,1,0:T(8,128)} %fusion.2) | data formatting | bytes 12582912 | tf_op jit(solution)/shard_map/reshape.8
  163.4 9.7 %convolution_bitcast_fusion = f32[16,128,2,128]{3,2,1,0:T(2,128)S(1)} fusion(f32[16,6,128,128]{3,1,2,0:T(8,128)} %copy.31, f32[16,6,2,1]{1,0,2,3:T(8,128)S(1)} %bitcast.37), kind=kOutput, calls=%fused_computation.5 | convolution fusion | flops 37748736 | bytes 8389376 | tf_op jit(solution)/shard_map/nspc,nspik->nick/dot_general | solution.py:51
  173.1 2.7 %reshape_reshape_reshape.3 = f32[4,512,256]{2,1,0:T(8,128)} reshape(f32[16,128,2,128]{3,2,1,0:T(2,128)S(1)} %convolution_bitcast_fusion) | data formatting | bytes 4194304 | tf_op jit(solution)/shard_map/reshape;reshape;reshape | solution.py:14
  175.8 29.9 %all_to_all.5 = f32[4,512,256]{2,1,0:T(8,128)S(1)} all-to-all(f32[4,512,256]{2,1,0:T(8,128)} %reshape_reshape_reshape.3), channel_id=1, replica_groups=mesh['gx'=8,'gy'=16,'gz'=4] {'gz'}, dimensions={0} | all-to-all | bytes 4194304 | tf_op jit(solution)/shard_map/all_to_all | solution.py:20
  205.7 1.0 reduce_sum.9
  (2 shorter events, 0.0 us)
Async XLA Ops:
  6.5 76.8 %all-gather.3.cloned.1.call-start = ((), (), s32[]{:S(2)}) async-start(), calls=%async_computation.1 | async-start | bytes 4456448 | tf_op jit(solution)/shard_map/all_gather | solution.py:39
  7.3 133.0 %all-gather.5.cloned.1.call-start = ((), (), s32[]{:S(2)}) async-start(), calls=%async_computation.2 | async-start | bytes 7077888 | tf_op jit(solution)/shard_map/all_gather | solution.py:44
Sparse Core Ops, SparseCore 0:
  9.4 73.9 all-gather.2
  85.5 54.7 all-gather.4
where the time goes:
time: 214 us; the launch traced here: 213 us
  waiting for transfers between devices  79.6 us (37%)
  blocking collectives  72.9 us (34%)
  matrix products  24.4 us (11%)
  local copies, waits for them, and re-layouts  17.9 us (8%)
  between operations  13.4 us (6%)
  other arithmetic  5.24 us (2%)
    all_gather x1, waiting for transfers between devices, body(): tile_part = lax.all_gather(a_masked, 'gx', axis=1, tiled=True)  51.1 us
    all_to_all x1, blocking collectives, sent_and_summed(): lax.all_to_all(blocks, axis, split_axis=0, concat_axis=0, tiled=True)  29.9 us
    all_gather x1, blocking collectives, body(): lax.all_gather(weights, 'gy', axis=1, tiled=True)  28.2 us
    all_gather x1, waiting for transfers between devices, body(): lax.all_gather(p_vals, 'gy', axis=1, tiled=True)  27.7 us
    all_gather x1, blocking collectives, body(): columns = lax.all_gather(a_cols, 'gx', axis=1, tiled=True)  14.8 us
    dot_general x1, matrix products, body(): jnp.einsum('nsij,nspjk->nspik', block_tile_part, chosen, precision=HIGHEST)  14.8 us
    dot_general x1, matrix products, body(): jnp.einsum('nspc,nspik->nick', weights_all[indices], product, precision=H...  9.66 us
    another operation x2, local copies, waits for them, and re-layouts  8.47 us
  transfers between devices with their start and end apart: 2, of which 2 were waited for; matrix products, arithmetic and copies ran while one was open for 5% of the time, Pallas kernels for 0%

commit v1 on v0

v1 whole, which is shorter than its diff:
```python
import jax
import jax.numpy as jnp
from jax import lax
from jax.experimental import pallas as pl
from jax.experimental.pallas import tpu as pltpu
from jax.sharding import PartitionSpec as P

MESH = pl.DeviceIdType.MESH
T = 128
NY = 4
NC = 2
NZ = 16
NX = 4
SLOTS = 6
ROWS_DEV = 2
TILES_A = ROWS_DEV * SLOTS
UNIT = 3
UNITS = TILES_A // UNIT
TILES_P = 4
PROWS = TILES_P * T + 8
HALF = NZ // 2
BF = jnp.bfloat16
F32 = jnp.float32


def kernel(
    a_hbm, ac, an, p_hbm, pc, pn, out_hbm,
    abuf, ameta, ameta_s, pbuf, phi, plo, cbuf, far, near,
    own_sem, p_send, p_recv, a_send, a_recv, m_send, m_recv,
    sib_send, sib_recv, smeta_recv, c_send, far_recv, near_recv, out_sem, meta_sem, go_sem,
):
    gx, me, x = lax.axis_index("gx"), lax.axis_index("gy"), lax.axis_index("gz")
    y, core = gx // NC, gx % NC

    def wrap(value, n):
        return lax.rem(value + 2 * n, n)

    def y_dev(d):
        return {"gx": wrap(y + d, NY) * NC + core}

    def y_slot(d):
        return wrap(y + d, NY) * NC + core

    sibling = {"gx": y * NC + 1 - core}

    def sib_slot(d):
        return wrap(y + d, NY) * NC + 1 - core

    def remote(src, dst, send, recv, device):
        return pltpu.make_async_remote_copy(
            src_ref=src, dst_ref=dst, send_sem=send, recv_sem=recv, device_id=device, device_id_type=MESH
        )

    own_a = pltpu.make_async_copy(a_hbm, abuf.at[gx], own_sem.at[0])
    own_p = pltpu.make_async_copy(p_hbm, pbuf.at[me, pl.ds(0, TILES_P * T)], own_sem.at[1])
    own_a.start()
    own_p.start()

    barrier = pltpu.get_barrier_semaphore()
    peers = [sibling, y_dev(1), y_dev(-1), {"gy": wrap(me + 1, NZ)}, {"gy": wrap(me - 1, NZ)}, {"gz": wrap(x + 1, NX)}, {"gz": wrap(x - 1, NX)}]
    for peer in peers:
        pl.semaphore_signal(barrier, inc=1, device_id=peer, device_id_type=MESH)

    row8 = lax.broadcasted_iota(jnp.int32, (8, T), 0)
    lane8 = lax.broadcasted_iota(jnp.int32, (8, T), 1)
    pmeta = jnp.zeros((8, T), F32)
    for t in range(TILES_P):
        live = pn[0, t, 0] > 0
        for col in range(2):
            weight = jnp.where(jnp.logical_and(live, pc[0, t, 0, 0] == col), 1.0, 0.0).astype(F32)
            pmeta = jnp.where(row8 == col * TILES_P + t, weight, pmeta)
    pbuf[me, TILES_P * T :, :] = pmeta
    meta = jnp.zeros((8, T), jnp.int32)
    for r in range(ROWS_DEV):
        for s in range(SLOTS):
            target = jnp.where(s < an[0, r, 0], ac[0, r, 0, s], NZ * TILES_P)
            meta = jnp.where(lane8 == r * SLOTS + s, target, meta)
    ameta[gx] = meta
    phi[NZ * TILES_P] = jnp.zeros((T, 2 * T), BF)
    plo[NZ * TILES_P] = jnp.zeros((T, 2 * T), BF)

    pl.semaphore_wait(barrier, len(peers))

    def a_part(slot, u, n=1):
        return abuf.at[slot, pl.ds(u * UNIT, n * UNIT)]

    ORDER = {1: (0, 1, 2, 3), -1: (2, 3, 0, 1)}
    EARLY = {1: (0, 1), -1: (2, 3)}
    LATE = {1: (2, 3), -1: (0, 1)}
    DIR = {1: 0, -1: 1}

    def a_first(d, u, slot):
        return remote(a_part(slot, u), a_part(slot, u), a_send.at[DIR[d], 0], a_recv.at[DIR[d], 0, u], y_dev(d))

    def a_second(d, u, slot):
        return remote(a_part(slot, u), a_part(slot, u), a_send.at[DIR[d], 1], a_recv.at[DIR[d], 1, u], y_dev(d))

    def m_first(d, slot):
        return remote(ameta.at[slot], ameta.at[slot], m_send.at[DIR[d]], m_recv.at[DIR[d]], y_dev(d))

    def m_second(slot):
        return remote(ameta.at[slot], ameta.at[slot], m_send.at[2], m_recv.at[2], y_dev(1))

    def to_sibling(kind, u, slot):
        return remote(a_part(slot, u), a_part(slot, u), sib_send.at[0], sib_recv.at[kind, u], sibling)

    def m_sibling(kind, slot):
        return remote(ameta.at[slot], ameta.at[slot], sib_send.at[1], smeta_recv.at[kind], sibling)

    def a_start():
        own_a.wait()
        for i in range(UNITS):
            for d in (1, -1):
                a_first(d, ORDER[d][i], gx).start()
            if i == 0:
                for d in (1, -1):
                    m_first(d, gx).start()
        for u in range(UNITS):
            to_sibling(0, u, gx).start()
        m_sibling(0, gx).start()

    def a_early():
        for i in range(UNITS // 2):
            for d in (1, -1):
                u = EARLY[d][i]
                slot = y_slot(-d)
                a_first(d, u, slot).wait_recv()
                a_second(d, u, slot).start()
                to_sibling(1 + DIR[d], u, slot).start()
            if i == 0:
                for d in (1, -1):
                    slot = y_slot(-d)
                    m_first(d, slot).wait_recv()
                    if d == 1:
                        m_second(slot).start()
                    m_sibling(1 + DIR[d], slot).start()

    def a_late():
        for i in range(UNITS // 2):
            for d in (1, -1):
                u = LATE[d][i]
                slot = y_slot(-d)
                a_first(d, u, slot).wait_recv()
                to_sibling(1 + DIR[d], u, slot).start()

    def a_far():
        slot = y_slot(2)
        m_second(slot).wait_recv()
        m_sibling(3, slot).start()
        for i in range(UNITS // 2):
            for d in (1, -1):
                u = EARLY[d][i]
                a_second(d, u, slot).wait_recv()
                to_sibling(3, u, slot).start()

    def a_finish():
        for kind, d in ((0, 0), (1, -1), (2, 1), (3, 2)):
            slot = sib_slot(d)
            m_sibling(kind, slot).wait_recv()
            for u in range(UNITS):
                to_sibling(kind, u, slot).wait_recv()
        copy = pltpu.make_async_copy(ameta, ameta_s, meta_sem)
        copy.start()
        copy.wait()

    def a_drain():
        for d in (0, 1):
            pltpu.make_async_copy(abuf.at[0], abuf.at[0], a_send.at[d, 0]).wait()
            half = abuf.at[0, pl.ds(0, TILES_A // 2)]
            pltpu.make_async_copy(half, half, a_send.at[d, 1]).wait()
        for j in range(3):
            pltpu.make_async_copy(ameta.at[0], ameta.at[0], m_send.at[j]).wait()
        part = abuf.at[pl.ds(0, NY)]
        pltpu.make_async_copy(part, part, sib_send.at[0]).wait()
        part = ameta.at[pl.ds(0, NY)]
        pltpu.make_async_copy(part, part, sib_send.at[1]).wait()

    PIECES = (3, 0, 1, 2)
    LAST = {1: (0, 1), -1: (3, 2)}

    def p_part(slot, j):
        return pbuf.at[slot, pl.ds(j * T, T + 8 if j == TILES_P - 1 else T)]

    def p_copy(d, step, j, slot, last=False):
        part = p_part(slot, j)
        return remote(
            part, part, p_send.at[DIR[d], 1 if last else 0], p_recv.at[DIR[d], step - 1, j], {"gy": wrap(me + d, NZ)}
        )

    def convert(slot, j):
        p = pbuf[slot, j * T : (j + 1) * T, :]
        weights = pbuf[slot, TILES_P * T :, :].astype(BF)
        hi = p.astype(BF)
        lo = (p - hi.astype(F32)).astype(BF)
        k = slot * TILES_P + j
        for col in range(2):
            weight = weights[col * TILES_P + j : col * TILES_P + j + 1, :]
            phi[k, :, col * T : (col + 1) * T] = hi * weight
            plo[k, :, col * T : (col + 1) * T] = lo * weight

    def p_start():
        own_p.wait()
        for j in PIECES:
            for d in (1, -1):
                p_copy(d, 1, j, me).start()
        for j in range(TILES_P):
            convert(me, j)

    def p_steps(first, last):
        def step(s, carry):
            for j in PIECES:
                for d in (1, -1):
                    slot = wrap(me - d * s, NZ)
                    p_copy(d, s, j, slot).wait_recv()
                    p_copy(d, s + 1, j, slot).start()
                for d in (1, -1):
                    convert(wrap(me - d * s, NZ), j)
            return carry

        lax.fori_loop(first, last + 1, step, 0)

    def p_seven():
        s = HALF - 1
        for j in PIECES:
            for d in (1, -1):
                slot = wrap(me - d * s, NZ)
                p_copy(d, s, j, slot).wait_recv()
                if j in LAST[d]:
                    p_copy(d, HALF, j, slot, last=True).start()
            for d in (1, -1):
                convert(wrap(me - d * s, NZ), j)

    def p_eight():
        slot = wrap(me + HALF, NZ)
        for i in range(TILES_P // 2):
            for d in (1, -1):
                p_copy(d, HALF, LAST[d][i], slot, last=True).wait_recv()
            for d in (1, -1):
                convert(slot, LAST[d][i])

    def p_drain():
        part = pbuf.at[pl.ds(0, HALF - 1)]
        for d in (1, -1):
            pltpu.make_async_copy(part, part, p_send.at[DIR[d], 0]).wait()
            rest = pbuf.at[0, pl.ds(0, 2 * T if d == 1 else 2 * T + 8)]
            pltpu.make_async_copy(rest, rest, p_send.at[DIR[d], 1]).wait()

    @pl.when(core == 0)
    def _():
        p_start()
        a_start()
        p_steps(1, 3)
        a_early()
        p_steps(4, HALF - 2)
        a_late()
        p_seven()
        pl.semaphore_signal(go_sem, inc=1, device_id=sibling, device_id_type=MESH)
        p_eight()
        a_far()

    @pl.when(core == 1)
    def _():
        a_start()
        a_early()
        a_late()
        pl.semaphore_wait(go_sem, 1)
        p_start()
        p_steps(1, 2)
        a_far()
        p_steps(3, HALF - 2)
        p_seven()
        p_eight()

    a_finish()

    def compute(o, b):
        row = o * NX + b
        slot, r = row // ROWS_DEV, row % ROWS_DEV
        total = jnp.zeros((T, 2 * T), F32)
        for pair in range(SLOTS // 2):
            left, high, low = [], [], []
            for s in (2 * pair, 2 * pair + 1):
                k = ameta_s[slot, 0, r * SLOTS + s]
                left.append(abuf[slot, r * SLOTS + s])
                high.append(phi[k])
                low.append(plo[k])
            a = jnp.concatenate(left, axis=1)
            hi = a.astype(BF)
            lo = (a - hi.astype(F32)).astype(BF)
            high = jnp.concatenate(high, axis=0)
            low = jnp.concatenate(low, axis=0)
            total += jnp.dot(hi, high, preferred_element_type=F32)
            total += jnp.dot(lo, high, preferred_element_type=F32)
            total += jnp.dot(hi, low, preferred_element_type=F32)
        cbuf[row] = total

    def c_far(d, h, b):
        return remote(cbuf.at[wrap(x + 2, NX) * NX + b], far.at[DIR[d], h], c_send.at[DIR[d]], far_recv.at[DIR[d], h], {"gz": wrap(x + d, NX)})

    def c_near(d, b):
        return remote(cbuf.at[wrap(x + d, NX) * NX + b], near.at[DIR[d], b], c_send.at[DIR[d]], near_recv.at[DIR[d], b], {"gz": wrap(x + d, NX)})

    opposite, right, left = wrap(x + 2, NX), wrap(x + 1, NX), wrap(x - 1, NX)

    def far_rows(b, carry):
        compute(opposite, b)
        c_far(1, b, b).start()
        compute(opposite, b + 2)
        c_far(-1, b, b + 2).start()
        return carry

    lax.fori_loop(0, 2, far_rows, 0)

    def near_rows(b, carry):
        compute(right, b + 2)
        c_near(1, b + 2).start()
        compute(left, b)
        c_near(-1, b).start()
        return carry

    lax.fori_loop(0, 2, near_rows, 0)

    def near_more(b, carry):
        compute(right, b)
        compute(left, b + 2)
        return carry

    lax.fori_loop(0, 2, near_more, 0)

    def add_far(b, carry):
        c_far(1, b, b).wait_recv()
        cbuf[right * NX + b] += far[0, b]
        c_near(1, b).start()
        c_far(-1, b, b + 2).wait_recv()
        cbuf[left * NX + b + 2] += far[1, b]
        c_near(-1, b + 2).start()
        return carry

    lax.fori_loop(0, 2, add_far, 0)

    def own_rows(b, carry):
        compute(x, b)
        return carry

    lax.fori_loop(0, NX, own_rows, 0)

    for b in (0, 2, 1, 3):
        for d in (1, -1):
            c_near(d, b).wait_recv()
        cbuf[x * NX + b] += near[0, b] + near[1, b]
        pltpu.make_async_copy(cbuf.at[x * NX + b], out_hbm.at[pl.ds(b * T, T)], out_sem.at[b]).start()
    p_drain()
    a_drain()
    part = cbuf.at[pl.ds(0, 6)]
    for d in (0, 1):
        pltpu.make_async_copy(part, part, c_send.at[d]).wait()
    for b in range(NX):
        pltpu.make_async_copy(cbuf.at[x * NX + b], out_hbm.at[pl.ds(b * T, T)], out_sem.at[b]).wait()


def body(a_vals, a_cols, a_count, p_vals, p_cols, p_count):
    a = a_vals.reshape(TILES_A, T, T)
    p = p_vals.reshape(TILES_P * T, T)
    hbm = pl.BlockSpec(memory_space=pl.ANY)
    smem = pl.BlockSpec(memory_space=pltpu.SMEM)
    dma = pltpu.SemaphoreType.DMA
    return pl.pallas_call(
        kernel,
        out_shape=jax.ShapeDtypeStruct((NX * T, 2 * T), F32),
        in_specs=[hbm, smem, smem, hbm, smem, smem],
        out_specs=hbm,
        scratch_shapes=[
            pltpu.VMEM((NY * NC, TILES_A, T, T), F32),
            pltpu.VMEM((NY * NC, 8, T), jnp.int32),
            pltpu.SMEM((NY * NC, 8, T), jnp.int32),
            pltpu.VMEM((NZ, PROWS, T), F32),
            pltpu.VMEM((NZ * TILES_P + 1, T, 2 * T), BF),
            pltpu.VMEM((NZ * TILES_P + 1, T, 2 * T), BF),
            pltpu.VMEM((NX * NX, T, 2 * T), F32),
            pltpu.VMEM((2, 2, T, 2 * T), F32),
            pltpu.VMEM((2, NX, T, 2 * T), F32),
            dma((2,)),
            dma((2, 2)),
            dma((2, HALF, TILES_P)),
            dma((2, 2)),
            dma((2, 2, UNITS)),
            dma((3,)),
            dma((3,)),
            dma((2,)),
            dma((4, UNITS)),
            dma((4,)),
            dma((2,)),
            dma((2, 2)),
            dma((2, NX)),
            dma((NX,)),
            dma,
            pltpu.SemaphoreType.REGULAR,
        ],
        compiler_params=pltpu.CompilerParams(collective_id=0, has_side_effects=True, vmem_limit_bytes=60 * 1024 * 1024),
    )(a, a_cols, a_count, p, p_cols, p_count)


def solution(mesh):
    placed = (
        P("gy", "gx", "gz", None, None, None),
        P("gy", "gx", "gz", None),
        P("gy", "gx", "gz"),
        P("gz", "gy", "gx", None, None, None),
        P("gz", "gy", "gx", None),
        P("gz", "gy", "gx"),
    )
    return jax.shard_map(body, mesh=mesh, in_specs=placed, out_specs=P(("gy", "gz"), "gx"), check_vma=False)
```

time: 214 us -> 86.7 us (0.41)
  Pallas kernels: 0 us -> 82 us
  waiting for transfers between devices: 79.6 us -> 0 us
  blocking collectives: 72.9 us -> 0 us
  matrix products: 24.4 us -> 0 us
  between operations: 13.4 us -> 0.01 us
  local copies, waits for them, and re-layouts: 17.9 us -> 4.52 us
  other arithmetic: 5.24 us -> 0 us
    pallas_call x0 -> x1, Pallas kernels: none -> 82 us  [body(): pl.pallas_call(kernel, out_shape=jax.ShapeDtypeStruct((NX * T, 2 * T), F3...]
    all_gather x2 -> x0, waiting for transfers between devices: 78.8 us -> none  [the longest x1 51.1 us: body(): tile_part = lax.all_gather(a_masked, 'gx', axis=1, tiled=True)]
    all_gather x2 -> x0, blocking collectives: 43 us -> none  [the longest x1 28.2 us: body(): lax.all_gather(weights, 'gy', axis=1, tiled=True)]
    all_to_all x1 -> x0, blocking collectives: 29.9 us -> none  [sent_and_summed(): lax.all_to_all(blocks, axis, split_axis=0, concat_axis=0, tiled=True)]
    dot_general x2 -> x0, matrix products: 24.4 us -> none  [the longest x1 14.8 us: body(): jnp.einsum('nsij,nspjk->nspik', block_tile_part, chosen, precision=HIGHEST)]
    another operation x3 -> x0, local copies, waits for them, and re-layouts: 11.2 us -> none
    gather x3 -> x0, local copies, waits for them, and re-layouts: 6.47 us -> none  [the longest x1 5.79 us: body(): chosen = values_all[indices]]
    unnamed x0 -> x10, local copies, waits for them, and re-layouts: none -> 4.52 us
  transfers between devices with their start and end apart: 2 -> 0, of which waited for: 2 -> 0; matrix products, arithmetic and copies ran while one was open for 5% -> 0% of each run, Pallas kernels for 0% -> 0%
where the time goes in v1:
time: 86.7 us; the launch traced here: 86.5 us
  Pallas kernels  82 us (95%)
  local copies, waits for them, and re-layouts  4.52 us (5%)
    pallas_call x1, Pallas kernels, body(): pl.pallas_call(kernel, out_shape=jax.ShapeDtypeStruct((NX * T, 2 * T), F3...  82 us
    unnamed x10, local copies, waits for them, and re-layouts  4.52 us

profile of v1, /device:TPU:1, one launch (start us, length us, event | category | flops | bytes accessed | tf_op | source)
XLA Modules:
  0.0 86.5 jit_solution(2773081442080939005)
XLA Ops:
  0.0 0.0 copy-start.2
  0.0 0.7 copy-done.2
  0.7 0.0 copy-start
  0.7 0.7 copy.7.an
  1.3 0.0 copy-done
  1.3 0.0 copy-start.1
  1.3 0.7 copy.8.pc
  2.0 0.0 copy-done.1
  2.0 0.7 copy.9.pn
  2.7 82.0 %shard_map.64 = f32[512,256]{1,0:T(8,128)} custom-call(f32[12,128,128]{2,1,0:T(8,128)} %bitcast.2, s32[1,2,1,6]{3,2,1,0:T(1,128)} %ac.1, s32[1,2,1]{2,1,0:T(2,128)} %copy.7.an, f32[512,128]{1,0:T(8,128)} %bitcast.3, s32[1,4,1,1]{3,2,1,0:T(1,128)} %copy.8.pc, s32[1,4,1]{2,1,0:T(4,128)} %copy.9.pn), custom_call_target="tpu_custom_call" | custom-call | tf_op jit(solution)/shard_map/pallas_call | solution.py:367
  84.7 1.9 %copy.11 = f32[512,256]{1,0:T(8,128)} copy(f32[512,256]{1,0:T(8,128)} %shard_map.64) | data formatting | bytes 1048576
Async XLA Ops:
  0.0 0.7 copy-start.2
  0.7 0.7 copy-start
  1.3 0.7 copy-start.1

commit v2 on v1

v2 whole, which is shorter than its diff:
```python
import jax
import jax.numpy as jnp
from jax import lax
from jax.experimental import pallas as pl
from jax.experimental.pallas import tpu as pltpu
from jax.sharding import PartitionSpec as P

MESH = pl.DeviceIdType.MESH
T = 128
NY = 4
NC = 2
NZ = 16
NX = 4
SLOTS = 6
ROWS_DEV = 2
TILES_A = ROWS_DEV * SLOTS
UNIT = TILES_A // 2
TILES_P = 4
PROWS = TILES_P * T
HALF = NZ // 2
NP = 8
PIECE = TILES_P * T // NP
PLAN0 = ("P0", "A0", "M", 1, 2, 3, "go", 4, 5, "A1", 6, 7, "A2", 8, "A3")
PLAN1 = ("A0", "M", "wait", "P0", 1, 2, "A1", 3, 4, "A2", 5, 6, "A3", 7, 8)
BF = jnp.bfloat16
F32 = jnp.float32


def kernel(
    a_hbm, ac_hbm, an_hbm, p_hbm, pc_hbm, pn_hbm, out,
    abuf, ameta, ameta_s, ac, an, pc, pn, pbuf, pmeta, phi, plo, cbuf, far, near,
    own_sem, p_send, p_recv, pm_send, pm_recv, a_send, a_recv, m_send, m_recv,
    sib_send, sib_recv, smeta_recv, c_send, far_recv, near_recv, out_sem, int_sem, meta_sem, go_sem,
):
    gx, me, x = lax.axis_index("gx"), lax.axis_index("gy"), lax.axis_index("gz")
    y, core = gx // NC, gx % NC

    def wrap(value, n):
        return lax.rem(value + 2 * n, n)

    def y_dev(d):
        return {"gx": wrap(y + d, NY) * NC + core}

    def y_slot(d):
        return wrap(y + d, NY) * NC + core

    sibling = {"gx": y * NC + 1 - core}

    def sib_slot(d):
        return wrap(y + d, NY) * NC + 1 - core

    def remote(src, dst, send, recv, device):
        return pltpu.make_async_remote_copy(
            src_ref=src, dst_ref=dst, send_sem=send, recv_sem=recv, device_id=device, device_id_type=MESH
        )

    own_a = pltpu.make_async_copy(a_hbm, abuf.at[gx], own_sem.at[0])
    own_p = pltpu.make_async_copy(p_hbm, pbuf.at[me], own_sem.at[1])
    own_p.start()
    own_a.start()
    ints = [
        pltpu.make_async_copy(src, dst, int_sem.at[i])
        for i, (src, dst) in enumerate(((ac_hbm, ac), (an_hbm, an), (pc_hbm, pc), (pn_hbm, pn)))
    ]
    for copy in ints:
        copy.start()

    barrier = pltpu.get_barrier_semaphore()
    peers = [sibling, y_dev(1), y_dev(-1), {"gy": wrap(me + 1, NZ)}, {"gy": wrap(me - 1, NZ)}, {"gz": wrap(x + 1, NX)}, {"gz": wrap(x - 1, NX)}]
    for peer in peers:
        pl.semaphore_signal(barrier, inc=1, device_id=peer, device_id_type=MESH)

    pl.semaphore_wait(barrier, len(peers))

    DIR = {1: 0, -1: 1}
    EARLY = {1: 0, -1: 1}

    def a_part(slot, u):
        return abuf.at[slot, pl.ds(u * UNIT, UNIT)]

    def a_first(d, u, slot):
        return remote(a_part(slot, u), a_part(slot, u), a_send.at[DIR[d]], a_recv.at[DIR[d], u], y_dev(d))

    def a_second(d, slot):
        part = a_part(slot, EARLY[d])
        return remote(part, part, a_send.at[DIR[d]], a_recv.at[DIR[d], 2], y_dev(d))

    def m_copy(hop, d, slot):
        return remote(ameta.at[slot], ameta.at[slot], m_send, m_recv.at[hop], y_dev(d))

    def to_sibling(kind, slot, u=None):
        part = abuf.at[slot] if u is None else a_part(slot, u)
        return remote(part, part, sib_send, sib_recv.at[kind], sibling)

    def m_sibling(kind, slot):
        return remote(ameta.at[slot], ameta.at[slot], m_send, smeta_recv.at[kind], sibling)

    def a_start():
        own_a.wait()
        for i in range(2):
            for d in (1, -1):
                a_first(d, EARLY[d] if i == 0 else 1 - EARLY[d], gx).start()
        to_sibling(0, gx).start()

    def a_near():
        for d in (1, -1):
            a_first(d, EARLY[d], y_slot(-d)).wait_recv()
            a_second(d, y_slot(-d)).start()
        for d in (1, -1):
            m_copy(DIR[d], d, y_slot(-d)).wait_recv()
        m_copy(2, 1, y_slot(-1)).start()
        for d in (1, -1):
            a_first(d, 1 - EARLY[d], y_slot(-d)).wait_recv()
            to_sibling(1 + DIR[d], y_slot(-d)).start()
            m_sibling(1 + DIR[d], y_slot(-d)).start()

    def a_far():
        slot = y_slot(2)
        m_copy(2, 1, slot).wait_recv()
        m_sibling(3, slot).start()
        for d in (1, -1):
            a_second(d, slot).wait_recv()
        to_sibling(3, slot).start()

    def a_finish():
        for kind, d in ((0, 0), (1, -1), (2, 1), (3, 2)):
            m_sibling(kind, sib_slot(d)).wait_recv()
            to_sibling(kind, sib_slot(d)).wait_recv()
        copy = pltpu.make_async_copy(ameta, ameta_s, meta_sem)
        copy.start()
        copy.wait()

    def a_drain():
        for d in (0, 1):
            part = abuf.at[pl.ds(0, 3), pl.ds(0, UNIT)]
            pltpu.make_async_copy(part, part, a_send.at[d]).wait()
        part = abuf.at[pl.ds(0, NY)]
        pltpu.make_async_copy(part, part, sib_send).wait()
        part = ameta.at[pl.ds(0, 3 + NY)]
        pltpu.make_async_copy(part, part, m_send).wait()

    PIECES = tuple(range(NP))[::-1]
    LAST = {1: tuple(range(NP // 2)), -1: tuple(range(NP // 2, NP))[::-1]}

    def p_part(slot, j):
        return pbuf.at[slot, pl.ds(j * PIECE, PIECE)]

    def p_copy(d, step, j, slot):
        part = p_part(slot, j)
        return remote(
            part, part, p_send.at[DIR[d]], p_recv.at[DIR[d], step - 1, j], {"gy": wrap(me + d, NZ)}
        )

    def pm_copy(d, step, slot):
        part = pmeta.at[slot]
        return remote(part, part, pm_send.at[DIR[d]], pm_recv.at[DIR[d], step - 1], {"gy": wrap(me + d, NZ)})

    lane = lax.broadcasted_iota(jnp.int32, (TILES_P, T), 1)

    def convert(slot, t):
        p = pbuf[slot, t * T : (t + 1) * T, :]
        packed = pmeta[slot]
        turned = pltpu.roll(packed, T // 2, 1)
        low_half = lane < T // 2
        weights = (jnp.where(low_half, packed, turned), jnp.where(low_half, turned, packed))
        hi = p.astype(BF)
        lo = (p - hi.astype(F32)).astype(BF)
        k = slot * TILES_P + t
        for col in range(2):
            weight = weights[col][t : t + 1, :].astype(BF)
            phi[k, :, col * T : (col + 1) * T] = hi * weight
            plo[k, :, col * T : (col + 1) * T] = lo * weight

    def metas():
        for copy in ints:
            copy.wait()
        row4 = lax.broadcasted_iota(jnp.int32, (TILES_P, T), 0)
        weights = jnp.zeros((TILES_P, T), F32)
        for t in range(TILES_P):
            column = jnp.where(pn[0, t] > 0, pc[0, t], -1)
            named = jnp.where(lane < T // 2, 0, 1) == column
            weights = jnp.where(jnp.logical_and(row4 == t, named), 1.0, weights)
        pmeta[me] = weights
        lane8 = lax.broadcasted_iota(jnp.int32, (8, T), 1)
        targets = jnp.zeros((8, T), jnp.int32)
        for r in range(ROWS_DEV):
            for s in range(SLOTS):
                target = jnp.where(s < an[0, r], ac[0, r, 0, s], NZ * TILES_P)
                targets = jnp.where(lane8 == r * SLOTS + s, target, targets)
        ameta[gx] = targets
        phi[NZ * TILES_P] = jnp.zeros((T, 2 * T), BF)
        plo[NZ * TILES_P] = jnp.zeros((T, 2 * T), BF)
        for d in (1, -1):
            pm_copy(d, 1, me).start()
            m_copy(DIR[d], d, gx).start()
        m_sibling(0, gx).start()

    def p_start():
        own_p.wait()
        for j in PIECES:
            for d in (1, -1):
                p_copy(d, 1, j, me).start()

    PER = NP // TILES_P

    def p_steps(first, last):
        def step(s, carry):
            for i, j in enumerate(PIECES):
                for d in (1, -1):
                    slot = wrap(me - d * s, NZ)
                    p_copy(d, s, j, slot).wait_recv()
                    p_copy(d, s + 1, j, slot).start()
                if i % PER == 0:
                    for d in (1, -1):
                        convert(wrap(me - d * (s - 1), NZ), i // PER)
            for d in (1, -1):
                slot = wrap(me - d * s, NZ)
                pm_copy(d, s, slot).wait_recv()
                pm_copy(d, s + 1, slot).start()
            return carry

        lax.fori_loop(first, last + 1, step, 0)

    def p_seven():
        s = HALF - 1
        for i, j in enumerate(PIECES):
            for d in (1, -1):
                slot = wrap(me - d * s, NZ)
                p_copy(d, s, j, slot).wait_recv()
                if j in LAST[d]:
                    p_copy(d, HALF, j, slot).start()
            if i % PER == 0:
                for d in (1, -1):
                    convert(wrap(me - d * (s - 1), NZ), i // PER)
        for d in (1, -1):
            slot = wrap(me - d * s, NZ)
            pm_copy(d, s, slot).wait_recv()
            if d == -1:
                pm_copy(d, HALF, slot).start()
        for t in range(TILES_P):
            for d in (1, -1):
                convert(wrap(me - d * s, NZ), t)

    def p_eight():
        slot = wrap(me + HALF, NZ)
        pm_copy(-1, HALF, slot).wait_recv()
        for i in range(NP // 2):
            for d in (1, -1):
                p_copy(d, HALF, LAST[d][i], slot).wait_recv()
            if i % PER == PER - 1:
                for d in (1, -1):
                    convert(slot, LAST[d][i] // PER)

    def p_drain():
        part = pbuf.at[pl.ds(0, 2 * HALF - 1), pl.ds(0, 2 * T)]
        for d in (1, -1):
            pltpu.make_async_copy(part, part, p_send.at[DIR[d]]).wait()
            metas_sent = pmeta.at[pl.ds(0, HALF - 1 if d == 1 else HALF)]
            pltpu.make_async_copy(metas_sent, metas_sent, pm_send.at[DIR[d]]).wait()

    def go():
        pl.semaphore_signal(go_sem, inc=1, device_id=sibling, device_id_type=MESH)

    def follow(plan):
        acts = {
            "P0": p_start, "A0": a_start, "A1": a_near, "A2": a_far, "A3": a_finish, "M": metas,
            "go": go, "wait": lambda: pl.semaphore_wait(go_sem, 1),
            HALF - 1: p_seven, HALF: p_eight,
        }
        run = []
        for item in plan + (None,):
            if item in range(1, HALF - 1):
                run.append(item)
                continue
            if run:
                p_steps(run[0], run[-1])
                run = []
            if item is not None:
                acts[item]()

    @pl.when(core == 0)
    def _():
        follow(PLAN0)

    @pl.when(core == 1)
    def _():
        follow(PLAN1)

    def compute(o, b):
        row = o * NX + b
        slot, r = row // ROWS_DEV, row % ROWS_DEV
        total = jnp.zeros((T, 2 * T), F32)
        for pair in range(SLOTS // 2):
            left, high, low = [], [], []
            for s in (2 * pair, 2 * pair + 1):
                k = ameta_s[slot, 0, r * SLOTS + s]
                left.append(abuf[slot, r * SLOTS + s])
                high.append(phi[k])
                low.append(plo[k])
            a = jnp.concatenate(left, axis=1)
            hi = a.astype(BF)
            lo = (a - hi.astype(F32)).astype(BF)
            high = jnp.concatenate(high, axis=0)
            low = jnp.concatenate(low, axis=0)
            total += jnp.dot(hi, high, preferred_element_type=F32)
            total += jnp.dot(lo, high, preferred_element_type=F32)
            total += jnp.dot(hi, low, preferred_element_type=F32)
        cbuf[row] = total

    def c_far(d, h, b):
        return remote(cbuf.at[wrap(x + 2, NX) * NX + b], far.at[DIR[d], h], c_send.at[DIR[d]], far_recv.at[DIR[d], h], {"gz": wrap(x + d, NX)})

    def c_near(d, b):
        return remote(cbuf.at[wrap(x + d, NX) * NX + b], near.at[DIR[d], b], c_send.at[DIR[d]], near_recv.at[DIR[d], b], {"gz": wrap(x + d, NX)})

    opposite, right, left = wrap(x + 2, NX), wrap(x + 1, NX), wrap(x - 1, NX)

    def far_rows(b, carry):
        compute(opposite, b)
        compute(opposite, b + 2)
        c_far(1, b, b).start()
        c_far(-1, b, b + 2).start()
        return carry

    lax.fori_loop(0, 2, far_rows, 0)

    def near_rows(b, carry):
        compute(right, b + 2)
        compute(left, b)
        c_near(1, b + 2).start()
        c_near(-1, b).start()
        return carry

    lax.fori_loop(0, 2, near_rows, 0)

    def near_more(b, carry):
        compute(right, b)
        compute(left, b + 2)
        return carry

    lax.fori_loop(0, 2, near_more, 0)

    def add_far(b, carry):
        c_far(1, b, b).wait_recv()
        cbuf[right * NX + b] += far[0, b]
        c_near(1, b).start()
        c_far(-1, b, b + 2).wait_recv()
        cbuf[left * NX + b + 2] += far[1, b]
        c_near(-1, b + 2).start()
        return carry

    lax.fori_loop(0, 2, add_far, 0)

    def own_rows(b, carry):
        compute(x, b)
        return carry

    lax.fori_loop(0, NX, own_rows, 0)

    def out_copy(b):
        return pltpu.make_async_copy(cbuf.at[x * NX + b], out.at[pl.ds(b * T, T)], out_sem.at[b])

    for b in (0, 2, 1, 3):
        for d in (1, -1):
            c_near(d, b).wait_recv()
        cbuf[x * NX + b] += near[0, b] + near[1, b]
        out_copy(b).start()
    p_drain()
    a_drain()
    part = cbuf.at[pl.ds(0, 6)]
    for d in (0, 1):
        pltpu.make_async_copy(part, part, c_send.at[d]).wait()
    for b in range(NX):
        out_copy(b).wait()


def body(a_vals, a_cols, a_count, p_vals, p_cols, p_count):
    a = a_vals.reshape(TILES_A, T, T)
    p = p_vals.reshape(TILES_P * T, T)
    hbm = pl.BlockSpec(memory_space=pltpu.HBM)
    dma = pltpu.SemaphoreType.DMA
    return pl.pallas_call(
        kernel,
        out_shape=jax.ShapeDtypeStruct((NX * T, 2 * T), F32),
        in_specs=[hbm] * 6,
        out_specs=pl.BlockSpec(memory_space=pl.ANY),
        scratch_shapes=[
            pltpu.VMEM((NY * NC, TILES_A, T, T), F32),
            pltpu.VMEM((NY * NC, 8, T), jnp.int32),
            pltpu.SMEM((NY * NC, 8, T), jnp.int32),
            pltpu.SMEM((1, ROWS_DEV, 1, SLOTS), jnp.int32),
            pltpu.SMEM((1, ROWS_DEV), jnp.int32),
            pltpu.SMEM((1, TILES_P), jnp.int32),
            pltpu.SMEM((1, TILES_P), jnp.int32),
            pltpu.VMEM((NZ, PROWS, T), F32),
            pltpu.VMEM((NZ, TILES_P, T), F32),
            pltpu.VMEM((NZ * TILES_P + 1, T, 2 * T), BF),
            pltpu.VMEM((NZ * TILES_P + 1, T, 2 * T), BF),
            pltpu.VMEM((NX * NX, T, 2 * T), F32),
            pltpu.VMEM((2, 2, T, 2 * T), F32),
            pltpu.VMEM((2, NX, T, 2 * T), F32),
            dma((2,)),
            dma((2,)),
            dma((2, HALF, NP)),
            dma((2,)),
            dma((2, HALF)),
            dma((2,)),
            dma((2, 3)),
            dma,
            dma((3,)),
            dma,
            dma((4,)),
            dma((4,)),
            dma((2,)),
            dma((2, 2)),
            dma((2, NX)),
            dma((NX,)),
            dma((4,)),
            dma,
            pltpu.SemaphoreType.REGULAR,
        ],
        compiler_params=pltpu.CompilerParams(collective_id=0, has_side_effects=True, vmem_limit_bytes=36 * 1024 * 1024),
    )(*(pltpu.with_memory_space_constraint(v, pltpu.HBM) for v in (a, a_cols, a_count.reshape(1, ROWS_DEV), p, p_cols.reshape(1, TILES_P), p_count.reshape(1, TILES_P))))


def solution(mesh):
    placed = (
        P("gy", "gx", "gz", None, None, None),
        P("gy", "gx", "gz", None),
        P("gy", "gx", "gz"),
        P("gz", "gy", "gx", None, None, None),
        P("gz", "gy", "gx", None),
        P("gz", "gy", "gx"),
    )
    return jax.shard_map(body, mesh=mesh, in_specs=placed, out_specs=P(("gy", "gz"), "gx"), check_vma=False)
```

time: 86.7 us -> 77.1 us (0.89)
  Pallas kernels: 82 us -> 76.2 us
  local copies, waits for them, and re-layouts: 4.52 us -> 0.8 us
    pallas_call x1, Pallas kernels: 82 us -> 76.2 us  [body(): pl.pallas_call(kernel, out_shape=jax.ShapeDtypeStruct((NX * T, 2 * T), F3...]
    unnamed x10 -> x1, local copies, waits for them, and re-layouts: 4.52 us -> 0.8 us
where the time goes in v2:
time: 77.1 us; the launch traced here: 77 us
  Pallas kernels  76.2 us (99%)
  local copies, waits for them, and re-layouts  0.8 us (1%)
    pallas_call x1, Pallas kernels, body(): pl.pallas_call(kernel, out_shape=jax.ShapeDtypeStruct((NX * T, 2 * T), F3...  76.2 us

profile of v2, /device:TPU:1, one launch (start us, length us, event | category | flops | bytes accessed | tf_op | source)
XLA Modules:
  0.0 77.0 jit_solution(17090510241433596650)
XLA Ops:
  0.0 76.2 %shard_map.64 = f32[512,256]{1,0:T(8,128)S(1)} custom-call(f32[12,128,128]{2,1,0:T(8,128)} %bitcast.5, s32[1,2,1,6]{3,2,1,0:T(1,128)} %ac_hbm.1, s32[1,2]{1,0:T(1,128)} %bitcast.7, f32[512,128]{1,0:T(8,128)} %bitcast.6, s32[1,4]{1,0:T(1,128)} %bitcast.8, s32[1,4]{1,0:T(1,128)} %bitcast.9), custom_call_target="tpu_custom_call" | custom-call | tf_op jit(solution)/shard_map/pallas_call | solution.py:382
  76.2 0.8 %copy.8 = f32[512,256]{1,0:T(8,128)} copy(f32[512,256]{1,0:T(8,128)S(1)} %shard_map.64) | data formatting | bytes 1048576

commit v3 on v2

--- a/solution.py
+++ b/solution.py
@@ -19,9 +19,10 @@
 PROWS = TILES_P * T
 HALF = NZ // 2
 NP = 8
+DEPTH = 4
 PIECE = TILES_P * T // NP
-PLAN0 = ("P0", "A0", "M", 1, 2, 3, "go", 4, 5, "A1", 6, 7, "A2", 8, "A3")
-PLAN1 = ("A0", "M", "wait", "P0", 1, 2, "A1", 3, 4, "A2", 5, 6, "A3", 7, 8)
+PLAN0 = ("P", "A0", "M", 1, "go", 2, "go", 3, 4, "go", 5, "A1", 6, 7, "A2", 8, "A3")
+PLAN1 = ("A0", "M", "Pa", "Pb", "Pc", "A1", 1, 2, "A2", 3, 4, 5, "A3", 6, 7, 8)
 BF = jnp.bfloat16
 F32 = jnp.float32
 
@@ -30,7 +31,7 @@
     a_hbm, ac_hbm, an_hbm, p_hbm, pc_hbm, pn_hbm, out,
     abuf, ameta, ameta_s, ac, an, pc, pn, pbuf, pmeta, phi, plo, cbuf, far, near,
     own_sem, p_send, p_recv, pm_send, pm_recv, a_send, a_recv, m_send, m_recv,
-    sib_send, sib_recv, smeta_recv, c_send, far_recv, near_recv, out_sem, int_sem, meta_sem, go_sem,
+    sib_send, sib_recv, smeta_recv, c_send, far_recv, near_recv, out_sem, int_sem, meta_sem, go_sem, credit,
 ):
     gx, me, x = lax.axis_index("gx"), lax.axis_index("gy"), lax.axis_index("gz")
     y, core = gx // NC, gx % NC
@@ -45,14 +46,16 @@
         return wrap(y + d, NY) * NC + core
 
     sibling = {"gx": y * NC + 1 - core}
-
-    def sib_slot(d):
-        return wrap(y + d, NY) * NC + 1 - core
 
     def remote(src, dst, send, recv, device):
         return pltpu.make_async_remote_copy(
             src_ref=src, dst_ref=dst, send_sem=send, recv_sem=recv, device_id=device, device_id_type=MESH
         )
+
+    barrier = pltpu.get_barrier_semaphore()
+    peers = [sibling, y_dev(1), y_dev(-1), {"gy": wrap(me + 1, NZ)}, {"gy": wrap(me - 1, NZ)}, {"gz": wrap(x + 1, NX)}, {"gz": wrap(x - 1, NX)}]
+    for peer in peers:
+        pl.semaphore_signal(barrier, inc=1, device_id=peer, device_id_type=MESH)
 
     own_a = pltpu.make_async_copy(a_hbm, abuf.at[gx], own_sem.at[0])
     own_p = pltpu.make_async_copy(p_hbm, pbuf.at[me], own_sem.at[1])
@@ -65,11 +68,6 @@
     for copy in ints:
         copy.start()
 
-    barrier = pltpu.get_barrier_semaphore()
-    peers = [sibling, y_dev(1), y_dev(-1), {"gy": wrap(me + 1, NZ)}, {"gy": wrap(me - 1, NZ)}, {"gz": wrap(x + 1, NX)}, {"gz": wrap(x - 1, NX)}]
-    for peer in peers:
-        pl.semaphore_signal(barrier, inc=1, device_id=peer, device_id_type=MESH)
-
     pl.semaphore_wait(barrier, len(peers))
 
     DIR = {1: 0, -1: 1}
@@ -88,19 +86,19 @@
     def m_copy(hop, d, slot):
         return remote(ameta.at[slot], ameta.at[slot], m_send, m_recv.at[hop], y_dev(d))
 
-    def to_sibling(kind, slot, u=None):
-        part = abuf.at[slot] if u is None else a_part(slot, u)
-        return remote(part, part, sib_send, sib_recv.at[kind], sibling)
-
-    def m_sibling(kind, slot):
-        return remote(ameta.at[slot], ameta.at[slot], m_send, smeta_recv.at[kind], sibling)
+    def to_sibling(slot):
+        part = abuf.at[slot]
+        return remote(part, part, sib_send, sib_recv, sibling)
+
+    def m_sibling(slot):
+        return remote(ameta.at[slot], ameta.at[slot], m_send, smeta_recv, sibling)
 
     def a_start():
         own_a.wait()
         for i in range(2):
             for d in (1, -1):
                 a_first(d, EARLY[d] if i == 0 else 1 - EARLY[d], gx).start()
-        to_sibling(0, gx).start()
+        to_sibling(gx).start()
 
     def a_near():
         for d in (1, -1):
@@ -111,24 +109,25 @@
         m_copy(2, 1, y_slot(-1)).start()
         for d in (1, -1):
             a_first(d, 1 - EARLY[d], y_slot(-d)).wait_recv()
-            to_sibling(1 + DIR[d], y_slot(-d)).start()
-            m_sibling(1 + DIR[d], y_slot(-d)).start()
+            to_sibling(y_slot(-d)).start()
+            m_sibling(y_slot(-d)).start()
 
     def a_far():
         slot = y_slot(2)
         m_copy(2, 1, slot).wait_recv()
-        m_sibling(3, slot).start()
+        m_sibling(slot).start()
         for d in (1, -1):
             a_second(d, slot).wait_recv()
-        to_sibling(3, slot).start()
+        to_sibling(slot).start()
+
+    to_smem = pltpu.make_async_copy(ameta, ameta_s, meta_sem)
 
     def a_finish():
-        for kind, d in ((0, 0), (1, -1), (2, 1), (3, 2)):
-            m_sibling(kind, sib_slot(d)).wait_recv()
-            to_sibling(kind, sib_slot(d)).wait_recv()
-        copy = pltpu.make_async_copy(ameta, ameta_s, meta_sem)
-        copy.start()
-        copy.wait()
+        part = ameta.at[pl.ds(0, NY)]
+        pltpu.make_async_copy(part, part, smeta_recv).wait()
+        part = abuf.at[pl.ds(0, NY)]
+        pltpu.make_async_copy(part, part, sib_recv).wait()
+        to_smem.start()
 
     def a_drain():
         for d in (0, 1):
@@ -148,12 +147,12 @@
     def p_copy(d, step, j, slot):
         part = p_part(slot, j)
         return remote(
-            part, part, p_send.at[DIR[d]], p_recv.at[DIR[d], step - 1, j], {"gy": wrap(me + d, NZ)}
+            part, part, p_send.at[DIR[d]], p_recv.at[DIR[d], (step - 1) % DEPTH, j], {"gy": wrap(me + d, NZ)}
         )
 
     def pm_copy(d, step, slot):
         part = pmeta.at[slot]
-        return remote(part, part, pm_send.at[DIR[d]], pm_recv.at[DIR[d], step - 1], {"gy": wrap(me + d, NZ)})
+        return remote(part, part, pm_send.at[DIR[d]], pm_recv.at[DIR[d], (step - 1) % DEPTH], {"gy": wrap(me + d, NZ)})
 
     lane = lax.broadcasted_iota(jnp.int32, (TILES_P, T), 1)
 
@@ -181,30 +180,53 @@
             named = jnp.where(lane < T // 2, 0, 1) == column
             weights = jnp.where(jnp.logical_and(row4 == t, named), 1.0, weights)
         pmeta[me] = weights
-        lane8 = lax.broadcasted_iota(jnp.int32, (8, T), 1)
-        targets = jnp.zeros((8, T), jnp.int32)
+        lane1 = lax.broadcasted_iota(jnp.int32, (1, T), 1)
+        targets = jnp.zeros((1, T), jnp.int32)
         for r in range(ROWS_DEV):
             for s in range(SLOTS):
                 target = jnp.where(s < an[0, r], ac[0, r, 0, s], NZ * TILES_P)
-                targets = jnp.where(lane8 == r * SLOTS + s, target, targets)
+                targets = jnp.where(lane1 == r * SLOTS + s, target, targets)
         ameta[gx] = targets
         phi[NZ * TILES_P] = jnp.zeros((T, 2 * T), BF)
         plo[NZ * TILES_P] = jnp.zeros((T, 2 * T), BF)
         for d in (1, -1):
             pm_copy(d, 1, me).start()
             m_copy(DIR[d], d, gx).start()
-        m_sibling(0, gx).start()
+        m_sibling(gx).start()
+
+    def p_send_own(pieces):
+        for j in pieces:
+            for d in (1, -1):
+                p_copy(d, 1, j, me).start()
 
     def p_start():
         own_p.wait()
-        for j in PIECES:
-            for d in (1, -1):
-                p_copy(d, 1, j, me).start()
+        p_send_own(PIECES)
+
+    def p_begin(first, last):
+        def act():
+            if first == 0:
+                own_p.wait()
+            pl.semaphore_wait(go_sem, 1)
+            p_send_own(PIECES[first:last])
+
+        return act
 
     PER = NP // TILES_P
+
+    def spend():
+        for d in (1, -1):
+            pl.semaphore_wait(credit.at[DIR[d]], 1)
+
+    def give():
+        for d in (1, -1):
+            pl.semaphore_signal(
+                credit.at[DIR[d]], inc=1, device_id={"gy": wrap(me - d, NZ)}, device_id_type=MESH
+            )
 
     def p_steps(first, last):
         def step(s, carry):
+            pl.when(s >= DEPTH)(spend)
             for i, j in enumerate(PIECES):
                 for d in (1, -1):
                     slot = wrap(me - d * s, NZ)
@@ -217,12 +239,14 @@
                 slot = wrap(me - d * s, NZ)
                 pm_copy(d, s, slot).wait_recv()
                 pm_copy(d, s + 1, slot).start()
+            pl.when(s <= HALF - DEPTH)(give)
             return carry
 
         lax.fori_loop(first, last + 1, step, 0)
 
     def p_seven():
         s = HALF - 1
+        spend()
         for i, j in enumerate(PIECES):
             for d in (1, -1):
                 slot = wrap(me - d * s, NZ)
@@ -263,8 +287,8 @@
 
     def follow(plan):
         acts = {
-            "P0": p_start, "A0": a_start, "A1": a_near, "A2": a_far, "A3": a_finish, "M": metas,
-            "go": go, "wait": lambda: pl.semaphore_wait(go_sem, 1),
+            "P": p_start, "Pa": p_begin(0, 3), "Pb": p_begin(3, 6), "Pc": p_begin(6, NP), "A0": a_start, "A1": a_near, "A2": a_far, "A3": a_finish, "M": metas,
+            "go": go,
             HALF - 1: p_seven, HALF: p_eight,
         }
         run = []
@@ -313,6 +337,7 @@
     def c_near(d, b):
         return remote(cbuf.at[wrap(x + d, NX) * NX + b], near.at[DIR[d], b], c_send.at[DIR[d]], near_recv.at[DIR[d], b], {"gz": wrap(x + d, NX)})
 
+    to_smem.wait()
     opposite, right, left = wrap(x + 2, NX), wrap(x + 1, NX), wrap(x - 1, NX)
 
     def far_rows(b, carry):
@@ -358,7 +383,7 @@
     lax.fori_loop(0, NX, own_rows, 0)
 
     def out_copy(b):
-        return pltpu.make_async_copy(cbuf.at[x * NX + b], out.at[pl.ds(b * T, T)], out_sem.at[b])
+        return pltpu.make_async_copy(cbuf.at[x * NX + b], out.at[pl.ds(b * T, T)], out_sem)
 
     for b in (0, 2, 1, 3):
         for d in (1, -1):
@@ -370,8 +395,8 @@
     part = cbuf.at[pl.ds(0, 6)]
     for d in (0, 1):
         pltpu.make_async_copy(part, part, c_send.at[d]).wait()
-    for b in range(NX):
-        out_copy(b).wait()
+    part = cbuf.at[pl.ds(0, NX)]
+    pltpu.make_async_copy(part, part, out_sem).wait()
 
 
 def body(a_vals, a_cols, a_count, p_vals, p_cols, p_count):
@@ -386,8 +411,8 @@
         out_specs=pl.BlockSpec(memory_space=pl.ANY),
         scratch_shapes=[
             pltpu.VMEM((NY * NC, TILES_A, T, T), F32),
-            pltpu.VMEM((NY * NC, 8, T), jnp.int32),
-            pltpu.SMEM((NY * NC, 8, T), jnp.int32),
+            pltpu.VMEM((NY * NC, 1, T), jnp.int32),
+            pltpu.SMEM((NY * NC, 1, T), jnp.int32),
             pltpu.SMEM((1, ROWS_DEV, 1, SLOTS), jnp.int32),
             pltpu.SMEM((1, ROWS_DEV), jnp.int32),
             pltpu.SMEM((1, TILES_P), jnp.int32),
@@ -401,23 +426,24 @@
             pltpu.VMEM((2, NX, T, 2 * T), F32),
             dma((2,)),
             dma((2,)),
-            dma((2, HALF, NP)),
+            dma((2, DEPTH, NP)),
             dma((2,)),
-            dma((2, HALF)),
+            dma((2, DEPTH)),
             dma((2,)),
             dma((2, 3)),
             dma,
             dma((3,)),
             dma,
-            dma((4,)),
-            dma((4,)),
+            dma,
+            dma,
             dma((2,)),
             dma((2, 2)),
             dma((2, NX)),
-            dma((NX,)),
+            dma,
             dma((4,)),
             dma,
             pltpu.SemaphoreType.REGULAR,
+            pltpu.SemaphoreType.REGULAR((2,)),
         ],
         compiler_params=pltpu.CompilerParams(collective_id=0, has_side_effects=True, vmem_limit_bytes=36 * 1024 * 1024),
     )(*(pltpu.with_memory_space_constraint(v, pltpu.HBM) for v in (a, a_cols, a_count.reshape(1, ROWS_DEV), p, p_cols.reshape(1, TILES_P), p_count.reshape(1, TILES_P))))

time: 77.1 us -> 75.7 us (0.982)
  Pallas kernels: 76.2 us -> 74.8 us
    pallas_call x1, Pallas kernels: 76.2 us -> 74.8 us  [body(): pl.pallas_call(kernel, out_shape=jax.ShapeDtypeStruct((NX * T, 2 * T), F3...]
where the time goes in v3:
time: 75.7 us; the launch traced here: 75.6 us
  Pallas kernels  74.8 us (99%)
  local copies, waits for them, and re-layouts  0.8 us (1%)
    pallas_call x1, Pallas kernels, body(): pl.pallas_call(kernel, out_shape=jax.ShapeDtypeStruct((NX * T, 2 * T), F3...  74.8 us

profile of v3, /device:TPU:1, one launch (start us, length us, event | category | flops | bytes accessed | tf_op | source)
XLA Modules:
  0.0 75.6 jit_solution(5836403096429369687)
XLA Ops:
  0.0 74.8 %shard_map.64 = f32[512,256]{1,0:T(8,128)S(1)} custom-call(f32[12,128,128]{2,1,0:T(8,128)} %bitcast.5, s32[1,2,1,6]{3,2,1,0:T(1,128)} %ac_hbm.1, s32[1,2]{1,0:T(1,128)} %bitcast.7, f32[512,128]{1,0:T(8,128)} %bitcast.6, s32[1,4]{1,0:T(1,128)} %bitcast.8, s32[1,4]{1,0:T(1,128)} %bitcast.9), custom_call_target="tpu_custom_call" | custom-call | tf_op jit(solution)/shard_map/pallas_call | solution.py:407
  74.8 0.8 %copy.8 = f32[512,256]{1,0:T(8,128)} copy(f32[512,256]{1,0:T(8,128)S(1)} %shard_map.64) | data formatting | bytes 1048576

commit v4 on v3

--- a/solution.py
+++ b/solution.py
@@ -21,8 +21,8 @@
 NP = 8
 DEPTH = 4
 PIECE = TILES_P * T // NP
-PLAN0 = ("P", "A0", "M", 1, "go", 2, "go", 3, 4, "go", 5, "A1", 6, 7, "A2", 8, "A3")
-PLAN1 = ("A0", "M", "Pa", "Pb", "Pc", "A1", 1, 2, "A2", 3, 4, 5, "A3", 6, 7, 8)
+PLAN0 = ("P", "A0", "M", 1, "go", 2, 3, "go", 4, 5, "A1", 6, 7, "A2", 8, "A3")
+PLAN1 = ("Pa", "A0", "M", "Pb", "Pc", 1, "A1", 2, 3, "A2", 4, 5, "A3", 6, 7, 8)
 BF = jnp.bfloat16
 F32 = jnp.float32
 
@@ -203,11 +203,12 @@
         own_p.wait()
         p_send_own(PIECES)
 
-    def p_begin(first, last):
+    def p_begin(first, last, held=True):
         def act():
             if first == 0:
                 own_p.wait()
-            pl.semaphore_wait(go_sem, 1)
+            if held:
+                pl.semaphore_wait(go_sem, 1)
             p_send_own(PIECES[first:last])
 
         return act
@@ -287,7 +288,7 @@
 
     def follow(plan):
         acts = {
-            "P": p_start, "Pa": p_begin(0, 3), "Pb": p_begin(3, 6), "Pc": p_begin(6, NP), "A0": a_start, "A1": a_near, "A2": a_far, "A3": a_finish, "M": metas,
+            "P": p_start, "Pa": p_begin(0, 3, False), "Pb": p_begin(3, 6), "Pc": p_begin(6, NP), "A0": a_start, "A1": a_near, "A2": a_far, "A3": a_finish, "M": metas,
             "go": go,
             HALF - 1: p_seven, HALF: p_eight,
         }

time: 75.7 us -> 74.8 us (0.988)
  Pallas kernels: 74.8 us -> 73.8 us
    pallas_call x1, Pallas kernels: 74.8 us -> 73.8 us  [body(): pl.pallas_call(kernel, out_shape=jax.ShapeDtypeStruct((NX * T, 2 * T), F3...]
where the time goes in v4:
time: 74.8 us; the launch traced here: 74.7 us
  Pallas kernels  73.8 us (99%)
  local copies, waits for them, and re-layouts  0.8 us (1%)
    pallas_call x1, Pallas kernels, body(): pl.pallas_call(kernel, out_shape=jax.ShapeDtypeStruct((NX * T, 2 * T), F3...  73.8 us

profile of v4, /device:TPU:1, one launch (start us, length us, event | category | flops | bytes accessed | tf_op | source)
XLA Modules:
  0.0 74.7 jit_solution(6260163992421901332)
XLA Ops:
  0.0 73.8 %shard_map.64 = f32[512,256]{1,0:T(8,128)S(1)} custom-call(f32[12,128,128]{2,1,0:T(8,128)} %bitcast.5, s32[1,2,1,6]{3,2,1,0:T(1,128)} %ac_hbm.1, s32[1,2]{1,0:T(1,128)} %bitcast.7, f32[512,128]{1,0:T(8,128)} %bitcast.6, s32[1,4]{1,0:T(1,128)} %bitcast.8, s32[1,4]{1,0:T(1,128)} %bitcast.9), custom_call_target="tpu_custom_call" | custom-call | tf_op jit(solution)/shard_map/pallas_call | solution.py:408
  73.9 0.8 %copy.8 = f32[512,256]{1,0:T(8,128)} copy(f32[512,256]{1,0:T(8,128)S(1)} %shard_map.64) | data formatting | bytes 1048576

commit v5 on v4

--- a/solution.py
+++ b/solution.py
@@ -138,7 +138,7 @@
         part = ameta.at[pl.ds(0, 3 + NY)]
         pltpu.make_async_copy(part, part, m_send).wait()
 
-    PIECES = tuple(range(NP))[::-1]
+    PIECES = {1: tuple(range(NP)), -1: tuple(range(NP))[::-1]}
     LAST = {1: tuple(range(NP // 2)), -1: tuple(range(NP // 2, NP))[::-1]}
 
     def p_part(slot, j):
@@ -194,14 +194,14 @@
             m_copy(DIR[d], d, gx).start()
         m_sibling(gx).start()
 
-    def p_send_own(pieces):
-        for j in pieces:
-            for d in (1, -1):
-                p_copy(d, 1, j, me).start()
+    def p_send_own(first, last):
+        for i in range(first, last):
+            for d in (1, -1):
+                p_copy(d, 1, PIECES[d][i], me).start()
 
     def p_start():
         own_p.wait()
-        p_send_own(PIECES)
+        p_send_own(0, NP)
 
     def p_begin(first, last, held=True):
         def act():
@@ -209,7 +209,7 @@
                 own_p.wait()
             if held:
                 pl.semaphore_wait(go_sem, 1)
-            p_send_own(PIECES[first:last])
+            p_send_own(first, last)
 
         return act
 
@@ -228,9 +228,9 @@
     def p_steps(first, last):
         def step(s, carry):
             pl.when(s >= DEPTH)(spend)
-            for i, j in enumerate(PIECES):
+            for i in range(NP):
                 for d in (1, -1):
-                    slot = wrap(me - d * s, NZ)
+                    j, slot = PIECES[d][i], wrap(me - d * s, NZ)
                     p_copy(d, s, j, slot).wait_recv()
                     p_copy(d, s + 1, j, slot).start()
                 if i % PER == 0:
@@ -248,9 +248,9 @@
     def p_seven():
         s = HALF - 1
         spend()
-        for i, j in enumerate(PIECES):
-            for d in (1, -1):
-                slot = wrap(me - d * s, NZ)
+        for i in range(NP):
+            for d in (1, -1):
+                j, slot = PIECES[d][i], wrap(me - d * s, NZ)
                 p_copy(d, s, j, slot).wait_recv()
                 if j in LAST[d]:
                     p_copy(d, HALF, j, slot).start()

time: 74.8 us -> 74 us (0.989)
  Pallas kernels: 73.8 us -> 73 us
    pallas_call x1, Pallas kernels: 73.8 us -> 73 us  [body(): pl.pallas_call(kernel, out_shape=jax.ShapeDtypeStruct((NX * T, 2 * T), F3...]
where the time goes in v5:
time: 74 us; the launch traced here: 73.9 us
  Pallas kernels  73 us (99%)
  local copies, waits for them, and re-layouts  0.8 us (1%)
    pallas_call x1, Pallas kernels, body(): pl.pallas_call(kernel, out_shape=jax.ShapeDtypeStruct((NX * T, 2 * T), F3...  73 us

profile of v5, /device:TPU:1, one launch (start us, length us, event | category | flops | bytes accessed | tf_op | source)
XLA Modules:
  0.0 73.9 jit_solution(1718135722079226494)
XLA Ops:
  0.0 73.0 %shard_map.64 = f32[512,256]{1,0:T(8,128)S(1)} custom-call(f32[12,128,128]{2,1,0:T(8,128)} %bitcast.5, s32[1,2,1,6]{3,2,1,0:T(1,128)} %ac_hbm.1, s32[1,2]{1,0:T(1,128)} %bitcast.7, f32[512,128]{1,0:T(8,128)} %bitcast.6, s32[1,4]{1,0:T(1,128)} %bitcast.8, s32[1,4]{1,0:T(1,128)} %bitcast.9), custom_call_target="tpu_custom_call" | custom-call | tf_op jit(solution)/shard_map/pallas_call | solution.py:408
  73.1 0.8 %copy.8 = f32[512,256]{1,0:T(8,128)} copy(f32[512,256]{1,0:T(8,128)S(1)} %shard_map.64) | data formatting | bytes 1048576

commit v6 on v5

--- a/solution.py
+++ b/solution.py
@@ -19,7 +19,7 @@
 PROWS = TILES_P * T
 HALF = NZ // 2
 NP = 8
-DEPTH = 4
+DEPTH = 3
 PIECE = TILES_P * T // NP
 PLAN0 = ("P", "A0", "M", 1, "go", 2, 3, "go", 4, 5, "A1", 6, 7, "A2", 8, "A3")
 PLAN1 = ("Pa", "A0", "M", "Pb", "Pc", 1, "A1", 2, 3, "A2", 4, 5, "A3", 6, 7, 8)
@@ -288,7 +288,7 @@
 
     def follow(plan):
         acts = {
-            "P": p_start, "Pa": p_begin(0, 3, False), "Pb": p_begin(3, 6), "Pc": p_begin(6, NP), "A0": a_start, "A1": a_near, "A2": a_far, "A3": a_finish, "M": metas,
+            "P": p_start, "Pa": p_begin(0, 4, False), "Pb": p_begin(4, 6), "Pc": p_begin(6, NP), "A0": a_start, "A1": a_near, "A2": a_far, "A3": a_finish, "M": metas,
             "go": go,
             HALF - 1: p_seven, HALF: p_eight,
         }

time: 74 us -> 73.7 us (level)
  no operation moved by 1% of the time
where the time goes in v6:
time: 73.7 us; the launch traced here: 73.6 us
  Pallas kernels  72.8 us (99%)
  local copies, waits for them, and re-layouts  0.8 us (1%)
    pallas_call x1, Pallas kernels, body(): pl.pallas_call(kernel, out_shape=jax.ShapeDtypeStruct((NX * T, 2 * T), F3...  72.8 us

profile of v6, /device:TPU:1, one launch (start us, length us, event | category | flops | bytes accessed | tf_op | source)
XLA Modules:
  0.0 73.6 jit_solution(469556810104847939)
XLA Ops:
  0.0 72.8 %shard_map.64 = f32[512,256]{1,0:T(8,128)S(1)} custom-call(f32[12,128,128]{2,1,0:T(8,128)} %bitcast.5, s32[1,2,1,6]{3,2,1,0:T(1,128)} %ac_hbm.1, s32[1,2]{1,0:T(1,128)} %bitcast.7, f32[512,128]{1,0:T(8,128)} %bitcast.6, s32[1,4]{1,0:T(1,128)} %bitcast.8, s32[1,4]{1,0:T(1,128)} %bitcast.9), custom_call_target="tpu_custom_call" | custom-call | tf_op jit(solution)/shard_map/pallas_call | solution.py:408
  72.8 0.8 %copy.8 = f32[512,256]{1,0:T(8,128)} copy(f32[512,256]{1,0:T(8,128)S(1)} %shard_map.64) | data formatting | bytes 1048576
